TPU v7x, 8 devices: a whole 2x2x1 slice. The times are simulated.
8 devices in a mesh: rep: 1 (over z), dp: 8 (over x, y, core).
Axes of the slice: x: 2, y: 2, z: 1, core: 2. Of those that a mesh axis runs over, the one named last changes fastest.
Arguments:
- g_w_gate: bfloat16 [8, 2, 896, 2560], P(('rep', 'dp'))
- g_w_up: bfloat16 [8, 2, 896, 2560], P(('rep', 'dp'))
- g_w_down: bfloat16 [8, 2, 2560, 896], P(('rep', 'dp'))
- w_gate: bfloat16 [2, 896, 2560], replicated
- w_up: bfloat16 [2, 896, 2560], replicated
- w_down: bfloat16 [2, 2560, 896], replicated
- m_w_gate: float32 [2, 896, 2560], P(None, 'dp')
- m_w_up: float32 [2, 896, 2560], P(None, 'dp')
- m_w_down: float32 [2, 2560, 896], P(None, 'dp')
- v_w_gate: float32 [2, 896, 2560], P(None, 'dp')
- v_w_up: float32 [2, 896, 2560], P(None, 'dp')
- v_w_down: float32 [2, 2560, 896], P(None, 'dp')
Outputs:
- output 1: bfloat16 [2, 896, 2560], P('rep')
- output 2: bfloat16 [2, 896, 2560], P('rep')
- output 3: bfloat16 [2, 2560, 896], P('rep')
- output 4: float32 [2, 896, 2560], P('rep', 'dp')
- output 5: float32 [2, 896, 2560], P('rep', 'dp')
- output 6: float32 [2, 2560, 896], P('rep', 'dp')
- output 7: float32 [2, 896, 2560], P('rep', 'dp')
- output 8: float32 [2, 896, 2560], P('rep', 'dp')
- output 9: float32 [2, 2560, 896], P('rep', 'dp')
All inputs are finite; a program needn't handle non-finite values.
Results may differ from a plain program's by a relative error of at most 0.022.
Values are sent between devices in bfloat16 or wider.
A program may use at most 2 GiB of HBM per device.

v0:
```python
import jax
import jax.numpy as jnp
from jax import lax
from jax.sharding import PartitionSpec as P


def adamw(w, m, v, g):
    m = 0.9 * m + 0.1 * g
    v = 0.95 * v + 0.05 * g * g
    step = m * lax.rsqrt(v + 1e-8) + 0.1 * w
    return (w - 0.02 * step).astype(jnp.bfloat16), m, v


def solution(mesh):
    def step(*arrays):
        terms, weights, m, v = (arrays[i : i + 3] for i in (0, 3, 6, 9))
        gradients = [lax.psum_scatter(t[0], "dp", scatter_dimension=1, tiled=True).astype(jnp.float32) for t in terms]
        me = lax.axis_index("dp")
        own = [lax.dynamic_slice_in_dim(w, me * one.shape[1], one.shape[1], 1).astype(jnp.float32) for w, one in zip(weights, m, strict=True)]
        new = [adamw(w, m, v, g) for w, m, v, g in zip(own, m, v, gradients, strict=True)]
        whole = [lax.all_gather(one[0], "dp", axis=1, tiled=True) for one in new]
        return (*whole, *(one[1] for one in new), *(one[2] for one in new))

    all_of, cut = P(None, None, None), P(None, "dp", None)
    return jax.shard_map(
        step,
        mesh=mesh,
        in_specs=(P(("rep", "dp"), None, None, None),) * 3 + (all_of,) * 3 + (cut,) * 6,
        out_specs=(P("rep", None, None),) * 3 + (P("rep", "dp", None),) * 6,
        check_vma=False,
    )
```

profile of v0, /device:TPU:0, one launch (start us, length us, event | category | flops | bytes accessed | tf_op | source)
XLA Modules:
  0.0 412.5 jit_solution(326458058896191378)
XLA Ops:
  7.2 0.0 reduce-scatter.8.cloned.1.call-start
  7.2 0.7 reduce-scatter.8.cloned.1.call-update
  7.9 0.0 reduce-scatter.6.cloned.1.call-start
  8.0 0.7 reduce-scatter.6.cloned.1.call-update
  8.7 0.0 reduce-scatter.4.cloned.1.call-start
  8.7 0.0 copy-start
  8.7 0.7 reduce-scatter.4.cloned.1.call-update
  9.4 0.0 all-gather.8.cloned.1.call-start
  9.4 70.9 %reduce-scatter.8.cloned.1.call-done = bf16[2,320,896]{2,1,0:T(8,128)(2,1)} async-done(((bf16[2,2560,896]{2,1,0:T(8,128)(2,1)}), bf16[2,320,896]{2,1,0:T(8,128)(2,1)}) %reduce-scatter.8.cloned.1.call-update) | async-done | bytes 1146896 | tf_op jit(solution)/shard_map/reduce_scatter | solution.py:17
  80.4 0.0 copy-done
  80.4 5.5 %fusion.10 = (bf16[2,320,896]{2,1,0:T(8,128)(2,1)}, f32[2,320,896]{2,1,0:T(8,128)}, f32[2,320,896]{2,1,0:T(8,128)}) fusion(bf16[2,2560,896]{2,1,0:T(8,128)(2,1)} %param.17, s32[]{:T(128)S(6)} %select_n.8, bf16[2,320,896]{2,1,0:T(8,128)(2,1)} %reduce-scatter.8.cloned.1.call-done, f32[2,320,896]{2,1,0:T(8,128)S(1)} %copy-done, f32[2,320,896]{2,1,0:T(8,128)} %param.20), kind=kLoop, calls=%fused_computation.22 | loop fusion | flops 9175040 | bytes 12615684 | tf_op jit(solution)/shard_map/convert_element_type | solution.py:11
  85.9 0.0 all-gather.8.cloned.1.call-update
  85.9 0.0 all-gather.6.cloned.1.call-start
  86.0 64.0 %reduce-scatter.6.cloned.1.call-done = bf16[2,112,2560]{2,1,0:T(8,128)(2,1)} async-done(((bf16[2,896,2560]{2,1,0:T(8,128)(2,1)}), bf16[2,112,2560]{2,1,0:T(8,128)(2,1)}) %reduce-scatter.6.cloned.1.call-update) | async-done | bytes 1146896 | tf_op jit(solution)/shard_map/reduce_scatter | solution.py:17
  150.0 0.0 copy-start.1
  150.0 6.3 %fusion.6 = (bf16[2,112,2560]{2,1,0:T(8,128)(2,1)}, f32[2,112,2560]{2,1,0:T(8,128)}, f32[2,112,2560]{2,1,0:T(8,128)}) fusion(bf16[2,896,2560]{2,1,0:T(8,128)(2,1)} %param.16, s32[]{:T(128)S(6)} %select_n.7, bf16[2,112,2560]{2,1,0:T(8,128)(2,1)} %reduce-scatter.6.cloned.1.call-done, f32[2,112,2560]{2,1,0:T(8,128)} %param.22, f32[2,112,2560]{2,1,0:T(8,128)} %param.19), kind=kLoop, calls=%fused_computation.18 | loop fusion | flops 9175040 | bytes 12615684 | tf_op jit(solution)/shard_map/convert_element_type | solution.py:11
  156.3 0.0 all-gather.6.cloned.1.call-update
  156.3 0.0 all-gather.4.cloned.1.call-start
  156.4 63.2 %reduce-scatter.4.cloned.1.call-done = bf16[2,112,2560]{2,1,0:T(8,128)(2,1)} async-done(((bf16[2,896,2560]{2,1,0:T(8,128)(2,1)}), bf16[2,112,2560]{2,1,0:T(8,128)(2,1)}) %reduce-scatter.4.cloned.1.call-update) | async-done | bytes 1146896 | tf_op jit(solution)/shard_map/reduce_scatter | solution.py:17
  219.5 0.0 copy-done.1
  219.6 5.5 %fusion.2 = (bf16[2,112,2560]{2,1,0:T(8,128)(2,1)}, f32[2,112,2560]{2,1,0:T(8,128)}, f32[2,112,2560]{2,1,0:T(8,128)}) fusion(bf16[2,896,2560]{2,1,0:T(8,128)(2,1)} %param.15, s32[]{:T(128)S(6)} %select_n.7, bf16[2,112,2560]{2,1,0:T(8,128)(2,1)} %reduce-scatter.4.cloned.1.call-done, f32[2,112,2560]{2,1,0:T(8,128)S(1)} %copy-done.1, f32[2,112,2560]{2,1,0:T(8,128)} %param.18), kind=kLoop, calls=%fused_computation.14 | loop fusion | flops 9175040 | bytes 12615684 | tf_op jit(solution)/shard_map/convert_element_type | solution.py:11
  225.1 0.0 all-gather.4.cloned.1.call-update
  225.1 48.6 %all-gather.8.cloned.1.call-done = bf16[2,2560,896]{2,1,0:T(8,128)(2,1)} async-done(((bf16[2,320,896]{2,1,0:T(8,128)(2,1)}), bf16[2,2560,896]{2,1,0:T(8,128)(2,1)}) %all-gather.8.cloned.1.call-update) | async-done | bytes 9175056 | tf_op jit(solution)/shard_map/all_gather | solution.py:21
  273.7 54.1 %all-gather.6.cloned.1.call-done = bf16[2,896,2560]{2,1,0:T(8,128)(2,1)} async-done(((bf16[2,112,2560]{2,1,0:T(8,128)(2,1)}), bf16[2,896,2560]{2,1,0:T(8,128)(2,1)}) %all-gather.6.cloned.1.call-update) | async-done | bytes 9175056 | tf_op jit(solution)/shard_map/all_gather | solution.py:21
  327.8 54.1 %all-gather.4.cloned.1.call-done = bf16[2,896,2560]{2,1,0:T(8,128)(2,1)} async-done(((bf16[2,112,2560]{2,1,0:T(8,128)(2,1)}), bf16[2,896,2560]{2,1,0:T(8,128)(2,1)}) %all-gather.4.cloned.1.call-update) | async-done | bytes 9175056 | tf_op jit(solution)/shard_map/all_gather | solution.py:21
  381.9 7.8 %copy.24 = bf16[2,896,2560]{2,1,0:T(8,128)(2,1)} copy(bf16[2,896,2560]{2,1,0:T(8,128)(2,1)} %all-gather.4.cloned.1.call-done) | data formatting | bytes 18350080
  389.8 7.8 %copy.25 = bf16[2,896,2560]{2,1,0:T(8,128)(2,1)} copy(bf16[2,896,2560]{2,1,0:T(8,128)(2,1)} %all-gather.6.cloned.1.call-done) | data formatting | bytes 18350080
  397.6 8.0 %copy.26 = bf16[2,2560,896]{2,1,0:T(8,128)(2,1)} copy(bf16[2,2560,896]{2,1,0:T(8,128)(2,1)} %all-gather.8.cloned.1.call-done) | data formatting | bytes 18350080
Async XLA Ops:
  7.2 73.2 %reduce-scatter.8.cloned.1.call-start = ((), (), s32[]{:S(2)}) async-start(), calls=%async_computation.7 | async-start | bytes 10321920 | tf_op jit(solution)/shard_map/reduce_scatter | solution.py:17
  7.9 142.1 %reduce-scatter.6.cloned.1.call-start = ((), (), s32[]{:S(2)}) async-start(), calls=%async_computation.5 | async-start | bytes 10321920 | tf_op jit(solution)/shard_map/reduce_scatter | solution.py:17
  8.7 210.9 %reduce-scatter.4.cloned.1.call-start = ((), (), s32[]{:S(2)}) async-start(), calls=%async_computation.3 | async-start | bytes 10321920 | tf_op jit(solution)/shard_map/reduce_scatter | solution.py:17
  8.7 71.7 %copy-start = (f32[2,320,896]{2,1,0:T(8,128)S(1)}, f32[2,320,896]{2,1,0:T(8,128)}, u32[]{:S(2)}) copy-start(f32[2,320,896]{2,1,0:T(8,128)} %param.23) | copy-start | bytes 6881284
  9.4 264.3 %all-gather.8.cloned.1.call-start = ((), (), s32[]{:S(2)}) async-start(), calls=%async_computation.8 | async-start | bytes 10321920 | tf_op jit(solution)/shard_map/all_gather | solution.py:21
  85.9 241.9 %all-gather.6.cloned.1.call-start = ((), (), s32[]{:S(2)}) async-start(), calls=%async_computation.6 | async-start | bytes 10321920 | tf_op jit(solution)/shard_map/all_gather | solution.py:21
  150.0 69.6 %copy-start.1 = (f32[2,112,2560]{2,1,0:T(8,128)S(1)}, f32[2,112,2560]{2,1,0:T(8,128)}, u32[]{:S(2)}) copy-start(f32[2,112,2560]{2,1,0:T(8,128)} %param.21) | copy-start | bytes 6881284
  156.3 225.6 %all-gather.4.cloned.1.call-start = ((), (), s32[]{:S(2)}) async-start(), calls=%async_computation.4 | async-start | bytes 10321920 | tf_op jit(solution)/shard_map/all_gather | solution.py:21
Sparse Core Ops, SparseCore 0:
  11.5 68.8 reduce-scatter.7
  83.9 65.9 reduce-scatter.5
  153.5 65.9 reduce-scatter.3
  221.8 51.8 all-gather.7
  275.9 51.8 all-gather.5
  330.1 51.8 all-gather.3
where the time goes:
time: 413 us; the launch traced here: 412 us
  waiting for transfers between devices  357 us (86%)
  local copies, waits for them, and re-layouts  23.7 us (6%)
  other arithmetic  17.4 us (4%)
  between operations  14.1 us (3%)
    reduce_scatter x3, waiting for transfers between devices, step(): lax.psum_scatter(t[0], 'dp', scatter_dimension=1, tiled=True)  198 us
    all_gather x3, waiting for transfers between devices, step(): whole = [lax.all_gather(one[0], 'dp', axis=1, tiled=True) for one in new]  157 us
    unnamed x7, local copies, waits for them, and re-layouts  23.7 us
    convert_element_type x3, other arithmetic, adamw(): return ((w - 0.02 * step).astype(jnp.bfloat16), m, v)  17.4 us
  transfers between devices with their start and end apart: 6, of which 6 were waited for; matrix products, arithmetic and copies ran while one was open for 4% of the time, Pallas kernels for 0%

commit v1 on v0

v1 whole, which is shorter than its diff:
```python
import functools

import jax
import jax.numpy as jnp
from jax import lax
from jax.experimental import pallas as pl
from jax.experimental.pallas import tpu as pltpu
from jax.sharding import PartitionSpec as P

MESH = pl.DeviceIdType.MESH
F32, BF16 = jnp.float32, jnp.bfloat16

LOAD, RS1, RS2, FETCH, STEP, STORED, AG1, AG2, END = range(9)
LAG = (0, 1, 3, 4, 5, 6, 7, 9, 10)
CHUNK = {112: 16, 320: 64}
PIECE = {112: (16, 512), 320: (16, 896)}


def adamw(w, m, v, g):
    m = 0.9 * m + 0.1 * g
    v = 0.95 * v + 0.05 * g * g
    step = m * lax.rsqrt(v + 1e-8) + 0.1 * w
    return (w - 0.02 * step).astype(BF16), m, v


def kinds():
    return {
        "far": (2, (2, 2), BF16),
        "near": (6, (2, 2), BF16),
        "partner": (None, (2, 2, 2), BF16),
        "send1": (3, (2, 2), BF16),
        "recv1": (None, (2, 2), BF16),
        "send2": (3, (2,), BF16),
        "recv2": (None, (2,), BF16),
        "w_in": (2, (2,), BF16),
        "m_in": (2, (2,), F32),
        "v_in": (2, (2,), F32),
        "m_out": (2, (2,), F32),
        "v_out": (2, (2,), F32),
    }


SEMS = ("far", "near", "partner", "partner_s", "recv1", "recv1_s", "recv2", "recv2_s", "fetch", "stored",
        "ag1", "ag2", "ag3", "own_s", "own3_s", "fwd_s", "fwd3_s")


def kernel(order, *refs):
    g, w, m, v = (refs[i : i + 3] for i in (0, 3, 6, 9))
    new_w, new_m, new_v = (refs[i : i + 3] for i in (12, 15, 18))
    refs = list(refs[21:])
    blocks = sorted({one.shape[1] for one in m})
    buf = {rows: {name: refs.pop(0) for name in kinds()} for rows in blocks}
    sem = {rows: {name: refs.pop(0) for name in SEMS} for rows in blocks}

    me = lax.axis_index("dp")
    x, y, core = me // 4, (me // 2) % 2, me % 2
    near_x, near_y, partner = me + 4 - 8 * x, me + 2 - 4 * y, me + 1 - 2 * core

    barrier = pltpu.get_barrier_semaphore()
    for other in (near_x, near_y, partner):
        pl.semaphore_signal(barrier, inc=1, device_id={"dp": other}, device_id_type=MESH)
    pl.semaphore_wait(barrier, 3)

    first, second = (near_x, near_y), (near_y, near_x)

    def block(layer, f, s, c):
        fx, fy = (f, s) if layer == 0 else (s, f)
        return (x + fx - 2 * x * fx) * 4 + (y + fy - 2 * y * fy) * 2 + c

    def run(stage, i, j):
        rows, cols = m[i].shape[1:]
        tall = CHUNK[rows]
        n = rows // tall
        b, sm = buf[rows], sem[rows]

        def at(layer, f, s, c=core):
            return (layer, pl.ds(pl.multiple_of(block(layer, f, s, c) * rows + j * tall, tall), tall))

        def slot(name):
            count = b[name].shape[0]
            return j if count == n else lax.rem(j, count)

        def of(name):
            return b[name].at[slot(name)]

        def take(name, like):
            pltpu.make_async_copy(of(like), of(like), sm[name].at[j]).wait()

        def local(src, dst, name):
            pltpu.make_async_copy(src, dst, sm[name].at[j]).start()

        def remote(src, dst, sent, received, other):
            pltpu.make_async_remote_copy(
                src_ref=src, dst_ref=dst, send_sem=sm[sent].at[j], recv_sem=sm[received].at[j],
                device_id={"dp": other}, device_id_type=MESH,
            ).start()

        def pieces(body):
            tr, tc = PIECE[rows]
            across = cols // tc

            def one(k, _):
                r = pl.multiple_of((k // across) * tr, tr)
                c = pl.multiple_of(lax.rem(k, across) * tc, 128)
                body(r, (pl.ds(r, tr), pl.ds(c, tc)), pl.ds(c, tc), tr)
                return 0

            lax.fori_loop(0, (tall // tr) * across, one, 0)

        own_rows = pl.ds(pl.multiple_of(j * tall, tall), tall)

        if stage == LOAD:
            for layer in (0, 1):
                for s in (0, 1):
                    remote(g[i].at[at(layer, 1, s, 1 - core)], of("partner").at[layer, 0, s], "partner_s", "partner", partner)
            for layer in (0, 1):
                for s in (0, 1):
                    local(g[i].at[at(layer, 1, s)], of("far").at[layer, s], "far")
            for layer in (0, 1):
                for s in (0, 1):
                    remote(g[i].at[at(layer, 0, s, 1 - core)], of("partner").at[layer, 1, s], "partner_s", "partner", partner)
                    local(g[i].at[at(layer, 0, s)], of("near").at[layer, s], "near")

        if stage == RS1:
            take("far", "far")
            take("partner", "partner")
            far, other, out = of("far"), of("partner"), of("send1")
            for layer in (0, 1):
                for s in (0, 1):
                    def add(r, p, c, tr, layer=layer, s=s):
                        out[(layer, s, *p)] = (far[(layer, s, *p)].astype(F32) + other[(layer, 0, s, *p)].astype(F32)).astype(BF16)
                    pieces(add)
            take("partner_s", "partner")
            for layer in (0, 1):
                remote(out.at[layer], of("recv1").at[layer], "recv1_s", "recv1", first[layer])

        if stage == RS2:
            take("near", "near")
            take("recv1", "recv1")
            near, other, came, out = of("near"), of("partner"), of("recv1"), of("send2")
            for layer in (0, 1):
                def add(r, p, c, tr, layer=layer):
                    out[(layer, *p)] = (
                        near[(layer, 1, *p)].astype(F32) + other[(layer, 1, 1, *p)].astype(F32) + came[(layer, 1, *p)].astype(F32)
                    ).astype(BF16)
                pieces(add)
            take("recv1_s", "recv1")
            for layer in (0, 1):
                remote(out.at[layer], of("recv2").at[layer], "recv2_s", "recv2", second[layer])

        if stage == FETCH:
            for layer in (0, 1):
                local(w[i].at[at(layer, 0, 0)], of("w_in").at[layer], "fetch")
                local(m[i].at[layer, own_rows], of("m_in").at[layer], "fetch")
                local(v[i].at[layer, own_rows], of("v_in").at[layer], "fetch")

        if stage == STEP:
            take("recv2", "recv2")
            take("fetch", "w_in")
            take("fetch", "m_in")
            take("fetch", "v_in")
            near, other, came, last = of("near"), of("partner"), of("recv1"), of("recv2")
            w_in, m_in, v_in, m_out, v_out = (of(k) for k in ("w_in", "m_in", "v_in", "m_out", "v_out"))
            for layer in (0, 1):
                start = block(layer, 0, 0, core) * rows + j * tall

                def step(r, p, c, tr, layer=layer, start=start):
                    total = near[(layer, 0, *p)].astype(F32) + other[(layer, 1, 0, *p)].astype(F32)
                    total = total + came[(layer, 0, *p)].astype(F32) + last[(layer, *p)].astype(F32)
                    total = total.astype(BF16).astype(F32)
                    one = adamw(w_in[(layer, *p)].astype(F32), m_in[(layer, *p)], v_in[(layer, *p)], total)
                    new_w[i][layer, pl.ds(pl.multiple_of(start + r, 16), tr), c] = one[0]
                    m_out[(layer, *p)] = one[1]
                    v_out[(layer, *p)] = one[2]
                pieces(step)
            take("recv2_s", "recv2")
            for layer in (0, 1):
                local(m_out.at[layer], new_m[i].at[layer, own_rows], "stored")
                local(v_out.at[layer], new_v[i].at[layer, own_rows], "stored")
            for layer in (0, 1):
                mine = new_w[i].at[at(layer, 0, 0)]
                remote(mine, mine, "own_s", "ag1", second[layer])
                remote(mine, mine, "own_s", "ag2", first[layer])
                remote(mine, mine, "own3_s", "ag3", partner)

        if stage == STORED:
            take("stored", "m_out")
            take("stored", "v_out")

        if stage == AG1:
            take("ag1", "recv2")
            for layer in (0, 1):
                came = new_w[i].at[at(layer, 0, 1)]
                remote(came, came, "fwd_s", "ag2", first[layer])
                remote(came, came, "fwd_s", "ag3", partner)

        if stage == AG2:
            take("ag2", "recv1")
            for layer in (0, 1):
                for s in (0, 1):
                    came = new_w[i].at[at(layer, 1, s)]
                    remote(came, came, "fwd3_s", "ag3", partner)

        if stage == END:
            take("ag3", "partner")
            take("own_s", "recv1")
            take("own3_s", "recv2")
            take("fwd_s", "recv1")
            take("fwd3_s", "recv1")

    spans, count = [], 0
    for i in order:
        n = m[i].shape[1] // CHUNK[m[i].shape[1]]
        spans.append((i, count, count + n))
        count += n

    def body(t, _):
        for stage in (END, LOAD, RS1, RS2, FETCH, STORED, STEP, AG1, AG2):
            u = t - LAG[stage]
            for i, start, end in spans:
                @pl.when(jnp.logical_and(u >= start, u < end))
                def _(i=i, start=start, stage=stage, u=u):
                    run(stage, i, u - start)
        return 0

    lax.fori_loop(0, count + LAG[END], body, 0)


def copy_out(n, *refs):
    sem = refs[2 * n]
    copies = [pltpu.make_async_copy(src, dst, sem.at[k]) for k, (src, dst) in enumerate(zip(refs[:n], refs[n : 2 * n], strict=True))]
    for copy in copies:
        copy.start()
    for copy in copies:
        copy.wait()


def to_hbm(*arrays):
    n = len(arrays)
    return pl.pallas_call(
        functools.partial(copy_out, n),
        out_shape=tuple(jax.ShapeDtypeStruct(a.shape, a.dtype) for a in arrays),
        in_specs=[pl.BlockSpec(memory_space=pl.ANY)] * n,
        out_specs=(pl.BlockSpec(memory_space=pl.ANY),) * n,
        scratch_shapes=[pltpu.SemaphoreType.DMA((n,))],
        compiler_params=pltpu.CompilerParams(vmem_limit_bytes=2**20),
    )(*arrays)


def solution(mesh):
    def step(*arrays):
        terms, weights, m, v = (arrays[i : i + 3] for i in (0, 3, 6, 9))
        scratch, sems = [], []
        for rows, cols in sorted({one.shape[1:] for one in m}):
            tall = CHUNK[rows]
            n = rows // tall
            for slots, held, kind in kinds().values():
                scratch.append(pltpu.VMEM((min(slots or n, n), *held, tall, cols), kind))
            sems += [pltpu.SemaphoreType.DMA((n,))] * len(SEMS)
        out = pl.pallas_call(
            functools.partial(kernel, (0, 2, 1)),
            out_shape=tuple(pltpu.VMEM(one.shape, one.dtype) for one in weights)
            + tuple(jax.ShapeDtypeStruct(one.shape, one.dtype) for one in (*m, *v)),
            in_specs=[pl.BlockSpec(memory_space=pl.ANY)] * 12,
            out_specs=(pl.BlockSpec(memory_space=pltpu.VMEM),) * 3 + (pl.BlockSpec(memory_space=pl.ANY),) * 6,
            scratch_shapes=scratch + sems,
            compiler_params=pltpu.CompilerParams(collective_id=0, has_side_effects=True, vmem_limit_bytes=35 * 2**20),
        )(*(t[0] for t in terms), *weights, *m, *v)
        return (*(to_hbm(one)[0] for one in out[:3]), *out[3:])

    all_of, cut = P(None, None, None), P(None, "dp", None)
    return jax.shard_map(
        step,
        mesh=mesh,
        in_specs=(P(("rep", "dp"), None, None, None),) * 3 + (all_of,) * 3 + (cut,) * 6,
        out_specs=(P("rep", None, None),) * 3 + (P("rep", "dp", None),) * 6,
        check_vma=False,
    )
```

time: 413 us -> 258 us (0.62)
  waiting for transfers between devices: 357 us -> 0 us
  Pallas kernels: 0 us -> 244 us
  other arithmetic: 17.4 us -> 0 us
  between operations: 14.1 us -> 0.71 us
  local copies, waits for them, and re-layouts: 23.7 us -> 13.7 us
    pallas_call x0 -> x4, Pallas kernels: none -> 244 us  [the longest x1 232 us: step(): pl.pallas_call(functools.partial(kernel, (0, 2, 1)), out_shape=tuple((plt...]
    reduce_scatter x3 -> x0, waiting for transfers between devices: 198 us -> none  [step(): lax.psum_scatter(t[0], 'dp', scatter_dimension=1, tiled=True)]
    all_gather x3 -> x0, waiting for transfers between devices: 157 us -> none  [step(): whole = [lax.all_gather(one[0], 'dp', axis=1, tiled=True) for one in new]]
    convert_element_type x3 -> x0, other arithmetic: 17.4 us -> none  [adamw(): return ((w - 0.02 * step).astype(jnp.bfloat16), m, v)]
    unnamed x7 -> x18, local copies, waits for them, and re-layouts: 23.7 us -> 13.7 us
  transfers between devices with their start and end apart: 6 -> 0, of which waited for: 6 -> 0; matrix products, arithmetic and copies ran while one was open for 4% -> 0% of each run, Pallas kernels for 0% -> 0%
where the time goes in v1:
time: 258 us
  Pallas kernels  244 us (95%)
  local copies, waits for them, and re-layouts  13.7 us (5%)
    pallas_call x1, Pallas kernels, step(): pl.pallas_call(functools.partial(kernel, (0, 2, 1)), out_shape=tuple((plt...  232 us
    unnamed x18, local copies, waits for them, and re-layouts  13.7 us
    pallas_call x3, Pallas kernels, to_hbm(): pl.pallas_call(functools.partial(copy_out, n), out_shape=tuple((jax.Shape...  11.2 us

profile of v1, /device:TPU:0, one launch (start us, length us, event | category | flops | bytes accessed | tf_op | source)
XLA Modules:
  0.0 258.0 jit_solution(4088669392571896512)
XLA Ops:
  0.6 232.4 %shard_map.187 = (bf16[2,896,2560]{2,1,0:T(8,128)(2,1)S(1)}, bf16[2,896,2560]{2,1,0:T(8,128)(2,1)S(1)}, bf16[2,2560,896]{2,1,0:T(8,128)(2,1)S(1)}, f32[2,112,256...) custom-call(bf16[2,896,2560]{2,1,0:T(8,128)(2,1)} %bitcast.3, ...), custom_call_target="tpu_custom_call" | custom-call | tf_op jit(solution)/shard_map/pallas_call | solution.py:260
  233.0 3.7 %shard_map.188 = bf16[2,896,2560]{2,1,0:T(8,128)(2,1)} custom-call(bf16[2,896,2560]{2,1,0:T(8,128)(2,1)S(1)} %get-tuple-element.18.refs_0_), custom_call_target="tpu_custom_call" | custom-call | tf_op jit(solution)/shard_map/pallas_call | solution.py:240
  236.7 3.7 %shard_map.189 = bf16[2,896,2560]{2,1,0:T(8,128)(2,1)} custom-call(bf16[2,896,2560]{2,1,0:T(8,128)(2,1)S(1)} %get-tuple-element.19.refs_0_), custom_call_target="tpu_custom_call" | custom-call | tf_op jit(solution)/shard_map/pallas_call | solution.py:240
  240.4 0.0 copy-start.5
  240.4 3.9 %shard_map.190 = bf16[2,2560,896]{2,1,0:T(8,128)(2,1)} custom-call(bf16[2,2560,896]{2,1,0:T(8,128)(2,1)S(1)} %get-tuple-element.20.refs_0_), custom_call_target="tpu_custom_call" | custom-call | tf_op jit(solution)/shard_map/pallas_call | solution.py:240
  244.2 0.0 copy-done.5
  244.2 0.0 copy-start.4
  244.3 1.4 copy.27
  245.6 1.1 copy-done.4
  246.7 0.0 copy-start.3
  246.7 1.4 copy.28
  248.1 1.1 copy-done.3
  249.2 0.0 copy-start.2
  249.2 1.4 copy.29
  250.6 1.1 copy-done.2
  251.7 0.0 copy-start.1
  251.7 1.4 copy.30
  253.1 1.1 copy-done.1
  254.1 0.0 copy-start
  254.1 1.4 copy.31
  255.5 1.1 copy-done
  256.6 1.4 copy.32
Async XLA Ops:
  240.4 3.9 %copy-start.5 = (f32[2,112,2560]{2,1,0:T(8,128)S(1)}, f32[2,112,2560]{2,1,0:T(8,128)}, u32[]{:S(2)}) copy-start(f32[2,112,2560]{2,1,0:T(8,128)} %get-tuple-element.39) | copy-start | bytes 6881284
  244.2 2.5 copy-start.4
  246.7 2.5 copy-start.3
  249.2 2.5 copy-start.2
  251.7 2.5 copy-start.1
  254.1 2.5 copy-start

commit v2 on v1

--- a/solution.py
+++ b/solution.py
@@ -10,9 +10,10 @@
 MESH = pl.DeviceIdType.MESH
 F32, BF16 = jnp.float32, jnp.bfloat16
 
-LOAD, RS1, RS2, FETCH, STEP, STORED, AG1, AG2, END = range(9)
-LAG = (0, 1, 3, 4, 5, 6, 7, 9, 10)
-CHUNK = {112: 16, 320: 64}
+LOAD, RS1, RS2, FETCH, STEP, AG1, AG2, END = range(8)
+LAG = (0, 1, 3, 4, 5, 7, 9, 10)
+CHUNK = {112: 16, 320: 32}
+AHEAD = {"partner": 7, "recv1": 6, "recv2": 6}
 PIECE = {112: (16, 512), 320: (16, 896)}
 
 
@@ -27,20 +28,18 @@
     return {
         "far": (2, (2, 2), BF16),
         "near": (6, (2, 2), BF16),
-        "partner": (None, (2, 2, 2), BF16),
+        "partner": (AHEAD["partner"], (2, 2, 2), BF16),
         "send1": (3, (2, 2), BF16),
-        "recv1": (None, (2, 2), BF16),
+        "recv1": (AHEAD["recv1"], (2, 2), BF16),
         "send2": (3, (2,), BF16),
-        "recv2": (None, (2,), BF16),
+        "recv2": (AHEAD["recv2"], (2,), BF16),
         "w_in": (2, (2,), BF16),
         "m_in": (2, (2,), F32),
         "v_in": (2, (2,), F32),
-        "m_out": (2, (2,), F32),
-        "v_out": (2, (2,), F32),
     }
 
 
-SEMS = ("far", "near", "partner", "partner_s", "recv1", "recv1_s", "recv2", "recv2_s", "fetch", "stored",
+SEMS = ("far", "near", "partner", "partner_s", "recv1", "recv1_s", "recv2", "recv2_s", "fetch",
         "ag1", "ag2", "ag3", "own_s", "own3_s", "fwd_s", "fwd3_s")
 
 
@@ -51,6 +50,8 @@
     blocks = sorted({one.shape[1] for one in m})
     buf = {rows: {name: refs.pop(0) for name in kinds()} for rows in blocks}
     sem = {rows: {name: refs.pop(0) for name in SEMS} for rows in blocks}
+    credit = refs.pop(0)
+    total = sum(one.shape[1] // CHUNK[one.shape[1]] for one in m)
 
     me = lax.axis_index("dp")
     x, y, core = me // 4, (me // 2) % 2, me % 2
@@ -67,7 +68,19 @@
         fx, fy = (f, s) if layer == 0 else (s, f)
         return (x + fx - 2 * x * fx) * 4 + (y + fy - 2 * y * fy) * 2 + c
 
-    def run(stage, i, j):
+    def give(u, name, others):
+        @pl.when(u + AHEAD[name] < total)
+        def _():
+            for k, other in others:
+                pl.semaphore_signal(credit.at[k], inc=1, device_id={"dp": other}, device_id_type=MESH)
+
+    def spend(u, name, ks):
+        @pl.when(u >= AHEAD[name])
+        def _():
+            for k in ks:
+                pl.semaphore_wait(credit.at[k], 1)
+
+    def run(stage, i, j, u):
         rows, cols = m[i].shape[1:]
         tall = CHUNK[rows]
         n = rows // tall
@@ -110,6 +123,7 @@
         own_rows = pl.ds(pl.multiple_of(j * tall, tall), tall)
 
         if stage == LOAD:
+            spend(u, "partner", (0,))
             for layer in (0, 1):
                 for s in (0, 1):
                     remote(g[i].at[at(layer, 1, s, 1 - core)], of("partner").at[layer, 0, s], "partner_s", "partner", partner)
@@ -131,6 +145,7 @@
                         out[(layer, s, *p)] = (far[(layer, s, *p)].astype(F32) + other[(layer, 0, s, *p)].astype(F32)).astype(BF16)
                     pieces(add)
             take("partner_s", "partner")
+            spend(u, "recv1", (1, 2))
             for layer in (0, 1):
                 remote(out.at[layer], of("recv1").at[layer], "recv1_s", "recv1", first[layer])
 
@@ -160,32 +175,28 @@
             take("fetch", "m_in")
             take("fetch", "v_in")
             near, other, came, last = of("near"), of("partner"), of("recv1"), of("recv2")
-            w_in, m_in, v_in, m_out, v_out = (of(k) for k in ("w_in", "m_in", "v_in", "m_out", "v_out"))
+            w_in, m_in, v_in = (of(k) for k in ("w_in", "m_in", "v_in"))
             for layer in (0, 1):
                 start = block(layer, 0, 0, core) * rows + j * tall
 
                 def step(r, p, c, tr, layer=layer, start=start):
-                    total = near[(layer, 0, *p)].astype(F32) + other[(layer, 1, 0, *p)].astype(F32)
-                    total = total + came[(layer, 0, *p)].astype(F32) + last[(layer, *p)].astype(F32)
-                    total = total.astype(BF16).astype(F32)
-                    one = adamw(w_in[(layer, *p)].astype(F32), m_in[(layer, *p)], v_in[(layer, *p)], total)
+                    gsum = near[(layer, 0, *p)].astype(F32) + other[(layer, 1, 0, *p)].astype(F32)
+                    gsum = gsum + came[(layer, 0, *p)].astype(F32) + last[(layer, *p)].astype(F32)
+                    gsum = gsum.astype(BF16).astype(F32)
+                    one = adamw(w_in[(layer, *p)].astype(F32), m_in[(layer, *p)], v_in[(layer, *p)], gsum)
                     new_w[i][layer, pl.ds(pl.multiple_of(start + r, 16), tr), c] = one[0]
-                    m_out[(layer, *p)] = one[1]
-                    v_out[(layer, *p)] = one[2]
+                    here = pl.ds(pl.multiple_of(j * tall + r, 16), tr)
+                    new_m[i][layer, here, c] = one[1]
+                    new_v[i][layer, here, c] = one[2]
                 pieces(step)
             take("recv2_s", "recv2")
-            for layer in (0, 1):
-                local(m_out.at[layer], new_m[i].at[layer, own_rows], "stored")
-                local(v_out.at[layer], new_v[i].at[layer, own_rows], "stored")
+            give(u, "partner", ((0, partner),))
+            give(u, "recv1", ((1, near_x), (2, near_y)))
             for layer in (0, 1):
                 mine = new_w[i].at[at(layer, 0, 0)]
                 remote(mine, mine, "own_s", "ag1", second[layer])
                 remote(mine, mine, "own_s", "ag2", first[layer])
                 remote(mine, mine, "own3_s", "ag3", partner)
-
-        if stage == STORED:
-            take("stored", "m_out")
-            take("stored", "v_out")
 
         if stage == AG1:
             take("ag1", "recv2")
@@ -215,12 +226,12 @@
         count += n
 
     def body(t, _):
-        for stage in (END, LOAD, RS1, RS2, FETCH, STORED, STEP, AG1, AG2):
+        for stage in (END, LOAD, RS1, RS2, FETCH, STEP, AG1, AG2):
             u = t - LAG[stage]
             for i, start, end in spans:
                 @pl.when(jnp.logical_and(u >= start, u < end))
                 def _(i=i, start=start, stage=stage, u=u):
-                    run(stage, i, u - start)
+                    run(stage, i, u - start, u)
         return 0
 
     lax.fori_loop(0, count + LAG[END], body, 0)
@@ -259,14 +270,14 @@
             sems += [pltpu.SemaphoreType.DMA((n,))] * len(SEMS)
         out = pl.pallas_call(
             functools.partial(kernel, (0, 2, 1)),
-            out_shape=tuple(pltpu.VMEM(one.shape, one.dtype) for one in weights)
-            + tuple(jax.ShapeDtypeStruct(one.shape, one.dtype) for one in (*m, *v)),
+            out_shape=tuple(pltpu.VMEM(one.shape, one.dtype) for one in (*weights, *m, *v)),
             in_specs=[pl.BlockSpec(memory_space=pl.ANY)] * 12,
-            out_specs=(pl.BlockSpec(memory_space=pltpu.VMEM),) * 3 + (pl.BlockSpec(memory_space=pl.ANY),) * 6,
-            scratch_shapes=scratch + sems,
-            compiler_params=pltpu.CompilerParams(collective_id=0, has_side_effects=True, vmem_limit_bytes=35 * 2**20),
+            out_specs=(pl.BlockSpec(memory_space=pltpu.VMEM),) * 9,
+            scratch_shapes=[*scratch, *sems, pltpu.SemaphoreType.REGULAR((3,))],
+            compiler_params=pltpu.CompilerParams(collective_id=0, has_side_effects=True, vmem_limit_bytes=22 * 2**20),
         )(*(t[0] for t in terms), *weights, *m, *v)
-        return (*(to_hbm(one)[0] for one in out[:3]), *out[3:])
+        first, rest = to_hbm(*out[:2]), to_hbm(*out[2:])
+        return (*first, *rest)
 
     all_of, cut = P(None, None, None), P(None, "dp", None)
     return jax.shard_map(

time: 258 us -> 248 us (0.961)
  local copies, waits for them, and re-layouts: 13.7 us -> 0 us
  Pallas kernels: 244 us -> 248 us
    unnamed x18 -> x0, local copies, waits for them, and re-layouts: 13.7 us -> none
    pallas_call x3 -> x2, Pallas kernels: 11.2 us -> 14.6 us  [to_hbm(): pl.pallas_call(functools.partial(copy_out, n), out_shape=tuple((jax.Shape...]
where the time goes in v2:
time: 248 us
  Pallas kernels  248 us (100%)
    pallas_call x1, Pallas kernels, step(): pl.pallas_call(functools.partial(kernel, (0, 2, 1)), out_shape=tuple((plt...  233 us
    pallas_call x2, Pallas kernels, to_hbm(): pl.pallas_call(functools.partial(copy_out, n), out_shape=tuple((jax.Shape...  14.6 us

profile of v2, /device:TPU:0, one launch (start us, length us, event | category | flops | bytes accessed | tf_op | source)
XLA Modules:
  0.0 248.3 jit_solution(13502419494991866612)
XLA Ops:
  0.6 233.0 %shard_map.187 = (bf16[2,896,2560]{2,1,0:T(8,128)(2,1)S(1)}, bf16[2,896,2560]{2,1,0:T(8,128)(2,1)S(1)}, bf16[2,2560,896]{2,1,0:T(8,128)(2,1)S(1)}, f32[2,112,256...) custom-call(bf16[2,896,2560]{2,1,0:T(8,128)(2,1)} %bitcast.3, ...), custom_call_target="tpu_custom_call" | custom-call | tf_op jit(solution)/shard_map/pallas_call | solution.py:271
  233.6 6.7 %shard_map.188 = (bf16[2,896,2560]{2,1,0:T(8,128)(2,1)}, bf16[2,896,2560]{2,1,0:T(8,128)(2,1)}) custom-call(bf16[2,896,2560]{2,1,0:T(8,128)(2,1)S(1)} %get-tuple-element.27.refs_0_, bf16[2,896,2560]{2,1,0:T(8,128)(2,1)S(1)} %get-tuple-element.28.refs_1_), custom_call_target="tpu_custom_call" | custom-call | tf_op jit(solution)/shard_map/pallas_call | solution.py:251
  240.3 7.9 %shard_map.189 = (bf16[2,2560,896]{2,1,0:T(8,128)(2,1)}, f32[2,112,2560]{2,1,0:T(8,128)}, f32[2,112,2560]{2,1,0:T(8,128)}, f32[2,320,896]{2,1,0:T(8,128)}, f32[2...) custom-call(bf16[2,2560,896]{2,1,0:T(8,128)(2,1)S(1)} %get-tuple-element.31.refs_0_, ...), custom_call_target="tpu_custom_call" | custom-call | tf_op jit(solution)/shard_map/pallas_call | solution.py:251

commit v3 on v0

v3 whole, which is shorter than its diff:
```python
import functools

import jax
import jax.numpy as jnp
from jax import lax
from jax.experimental import pallas as pl
from jax.experimental.pallas import tpu as pltpu
from jax.sharding import PartitionSpec as P

MESH = pl.DeviceIdType.MESH
F32, BF16 = jnp.float32, jnp.bfloat16

LOAD, RS1, RS2, FETCH, STEP, AG1, AG2, END = range(8)
LAG = (0, 1, 3, 4, 5, 7, 9, 10)
ORDER = (END, LOAD, RS1, RS2, FETCH, STEP, AG1, AG2)
RUNS = ((2, 0, 1, 1), (0, 0, 1, 1), (1, 0, 1, 1))
CHUNK = {2560: 16, 896: 32}
AHEAD = {"partner": 7, "recv1": 6, "recv2": 6}
WIDE = 512

BUFFERS = {
    "far": (2, (2, 2), BF16),
    "near": (6, (2, 2), BF16),
    "partner": (AHEAD["partner"], (2, 2, 2), BF16),
    "send1": (3, (2, 2), BF16),
    "recv1": (AHEAD["recv1"], (2, 2), BF16),
    "send2": (3, (2,), BF16),
    "recv2": (AHEAD["recv2"], (2,), BF16),
    "w_in": (2, (2,), BF16),
    "m_in": (2, (2,), F32),
    "v_in": (2, (2,), F32),
}
SEMS = {"far": 7, "near": 7, "sent1": 4, "recv1": 6, "recv2": 6, "sent2": 3, "ag1": 5, "ag2": 9, "ag3": 10, "sent3": 5}


def adamw(w, m, v, g):
    m = 0.9 * m + 0.1 * g
    v = 0.95 * v + 0.05 * g * g
    step = m * lax.rsqrt(v + 1e-8) + 0.1 * w
    return (w - 0.02 * step).astype(BF16), m, v


def kernel(*refs):
    g, w, m, v = (refs[i : i + 3] for i in (0, 3, 6, 9))
    new_w, new_m, new_v = (refs[i : i + 3] for i in (12, 15, 18))
    refs = list(refs[21:])
    widths = sorted({one.shape[2] for one in m})
    buf = {cols: {name: refs.pop(0) for name in BUFFERS} for cols in widths}
    sem = {name: refs.pop(0) for name in SEMS}
    credit = refs.pop(0)

    spans, total, done = [], 0, dict.fromkeys(widths, 0)
    for i, start, end, parts in RUNS:
        rows, cols = m[i].shape[1:]
        n = rows // CHUNK[cols]
        a, b = n * start // parts, n * end // parts
        spans.append((i, total, total + b - a, a, done[cols]))
        total += b - a
        done[cols] += b - a

    me = lax.axis_index("dp")
    x, y, core = me // 4, (me // 2) % 2, me % 2
    near_x, near_y, partner = me + 4 - 8 * x, me + 2 - 4 * y, me + 1 - 2 * core
    first, second = (near_x, near_y), (near_y, near_x)

    barrier = pltpu.get_barrier_semaphore()
    for other in (partner, near_x, near_y):
        pl.semaphore_signal(barrier, inc=1, device_id={"dp": other}, device_id_type=MESH)
    pl.semaphore_wait(barrier, 3)

    def block(layer, f, s, c):
        fx, fy = (f, s) if layer == 0 else (s, f)
        return (x + fx - 2 * x * fx) * 4 + (y + fy - 2 * y * fy) * 2 + c

    def give(u, name, others):
        @pl.when(u + AHEAD[name] < total)
        def _():
            for k, other in others:
                pl.semaphore_signal(credit.at[k], inc=1, device_id={"dp": other}, device_id_type=MESH)

    def spend(u, name, ks):
        @pl.when(u >= AHEAD[name])
        def _():
            for k in ks:
                pl.semaphore_wait(credit.at[k], 1)

    def run(stage, i, j, u, pos):
        rows, cols = m[i].shape[1:]
        b = buf[cols]
        wide = WIDE if cols % WIDE == 0 else cols
        tall = CHUNK[cols]

        def at(layer, f, s, c=core):
            return (layer, pl.ds(pl.multiple_of(block(layer, f, s, c) * rows + j * tall, tall), tall))

        def of(name):
            return b[name].at[lax.rem(pos, b[name].shape[0])]

        def signal(name):
            return sem[name].at[lax.rem(u, sem[name].shape[0])]

        def take(name, chunks):
            like = g[i].at[0, pl.ds(0, chunks * tall)]
            pltpu.make_async_copy(like, like, signal(name)).wait()

        def local(src, dst, name):
            pltpu.make_async_copy(src, dst, signal(name)).start()

        def remote(src, dst, sent, received, other):
            pltpu.make_async_remote_copy(
                src_ref=src, dst_ref=dst, send_sem=signal(sent), recv_sem=signal(received),
                device_id={"dp": other}, device_id_type=MESH,
            ).start()

        def pieces(body):
            def one(k, _):
                body((slice(None), pl.ds(pl.multiple_of(k * wide, 128), wide)))
                return 0

            lax.fori_loop(0, cols // wide, one, 0)

        own = pl.ds(pl.multiple_of(j * tall, tall), tall)
        other = of("partner")

        if stage == LOAD:
            spend(u, "partner", (0,))
            for side, mine in ((1, "far"), (0, "near")):
                for layer in (0, 1):
                    for s in (0, 1):
                        remote(g[i].at[at(layer, side, s, 1 - core)], other.at[1 - side, layer, s], "sent1", mine, partner)
                for layer in (0, 1):
                    for s in (0, 1):
                        local(g[i].at[at(layer, side, s)], of(mine).at[layer, s], mine)

        if stage == RS1:
            far, out = of("far"), of("send1")
            take("far", 8)
            for layer in (0, 1):
                for s in (0, 1):
                    def add(p, layer=layer, s=s):
                        out[(layer, s, *p)] = (far[(layer, s, *p)].astype(F32) + other[(0, layer, s, *p)].astype(F32)).astype(BF16)
                    pieces(add)
            spend(u, "recv1", (1, 2))
            for layer in (0, 1):
                remote(out.at[layer], of("recv1").at[layer], "sent1", "recv1", first[layer])

        if stage == RS2:
            near, came, out = of("near"), of("recv1"), of("send2")
            take("near", 8)
            take("recv1", 4)
            for layer in (0, 1):
                def add(p, layer=layer):
                    out[(layer, *p)] = (
                        near[(layer, 1, *p)].astype(F32) + other[(1, layer, 1, *p)].astype(F32) + came[(layer, 1, *p)].astype(F32)
                    ).astype(BF16)
                pieces(add)
            take("sent1", 12)
            for layer in (0, 1):
                remote(out.at[layer], of("recv2").at[layer], "sent2", "recv2", second[layer])

        if stage == FETCH:
            for layer in (0, 1):
                local(w[i].at[at(layer, 0, 0)], of("w_in").at[layer], "recv2")
                local(m[i].at[layer, own], of("m_in").at[layer], "recv2")
                local(v[i].at[layer, own], of("v_in").at[layer], "recv2")

        if stage == STEP:
            near, came, last = of("near"), of("recv1"), of("recv2")
            w_in, m_in, v_in = of("w_in"), of("m_in"), of("v_in")
            take("recv2", 12)
            for layer in (0, 1):
                rows_of = at(layer, 0, 0)[1]

                def step(p, layer=layer, rows_of=rows_of):
                    gsum = near[(layer, 0, *p)].astype(F32) + other[(1, layer, 0, *p)].astype(F32)
                    gsum = gsum + came[(layer, 0, *p)].astype(F32) + last[(layer, *p)].astype(F32)
                    gsum = gsum.astype(BF16).astype(F32)
                    one = adamw(w_in[(layer, *p)].astype(F32), m_in[(layer, *p)], v_in[(layer, *p)], gsum)
                    new_w[i][layer, rows_of, p[1]] = one[0]
                    new_m[i][layer, own, p[1]] = one[1]
                    new_v[i][layer, own, p[1]] = one[2]
                pieces(step)
            take("sent2", 2)
            give(u, "partner", ((0, partner),))
            give(u, "recv1", ((1, near_x), (2, near_y)))
            for layer in (0, 1):
                mine = new_w[i].at[at(layer, 0, 0)]
                remote(mine, mine, "sent3", "ag1", second[layer])
                remote(mine, mine, "sent3", "ag2", first[layer])
                remote(mine, mine, "sent3", "ag3", partner)

        if stage == AG1:
            take("ag1", 2)
            for layer in (0, 1):
                came = new_w[i].at[at(layer, 0, 1)]
                remote(came, came, "sent3", "ag2", first[layer])
            for layer in (0, 1):
                came = new_w[i].at[at(layer, 0, 1)]
                remote(came, came, "sent3", "ag3", partner)

        if stage == AG2:
            take("ag2", 4)
            for layer in (0, 1):
                for s in (0, 1):
                    came = new_w[i].at[at(layer, 1, s)]
                    remote(came, came, "sent3", "ag3", partner)

        if stage == END:
            take("ag3", 8)
            take("sent3", 14)

    def body(t, _):
        for stage in ORDER:
            u = t - LAG[stage]
            for i, start, end, chunk, pos in spans:
                @pl.when(jnp.logical_and(u >= start, u < end))
                def _(i=i, start=start, chunk=chunk, pos=pos, stage=stage, u=u):
                    run(stage, i, u - start + chunk, u, u - start + pos)
        return 0

    lax.fori_loop(0, total + LAG[END], body, 0)


def copy_out(n, *refs):
    copies = [
        pltpu.make_async_copy(src.at[layer], dst.at[layer], refs[2 * n])
        for src, dst in zip(refs[:n], refs[n : 2 * n], strict=True) for layer in (0, 1)
    ]
    for copy in copies:
        copy.start()
    for copy in copies:
        copy.wait()


def to_hbm(*arrays):
    n = len(arrays)
    return pl.pallas_call(
        functools.partial(copy_out, n),
        out_shape=tuple(jax.ShapeDtypeStruct(a.shape, a.dtype) for a in arrays),
        in_specs=[pl.BlockSpec(memory_space=pl.ANY)] * n,
        out_specs=(pl.BlockSpec(memory_space=pl.ANY),) * n,
        scratch_shapes=[pltpu.SemaphoreType.DMA],
        compiler_params=pltpu.CompilerParams(vmem_limit_bytes=2**20),
    )(*arrays)


def solution(mesh):
    def step(*arrays):
        terms, weights, m, v = (arrays[i : i + 3] for i in (0, 3, 6, 9))
        widths = sorted({one.shape[2] for one in m})
        scratch = [pltpu.VMEM((slots, *held, CHUNK[cols], cols), kind) for cols in widths for slots, held, kind in BUFFERS.values()]
        sems = [pltpu.SemaphoreType.DMA((slots,)) for slots in SEMS.values()]
        out = pl.pallas_call(
            kernel,
            out_shape=tuple(pltpu.VMEM(one.shape, one.dtype) for one in (*weights, *m, *v)),
            in_specs=[pl.BlockSpec(memory_space=pl.ANY)] * 12,
            out_specs=(pl.BlockSpec(memory_space=pltpu.VMEM),) * 9,
            scratch_shapes=[*scratch, *sems, pltpu.SemaphoreType.REGULAR((3,))],
            compiler_params=pltpu.CompilerParams(collective_id=0, has_side_effects=True, vmem_limit_bytes=22 * 2**20),
        )(*(t[0] for t in terms), *weights, *m, *v)
        return (*to_hbm(*out[:2]), *to_hbm(*out[2:]))

    all_of, cut = P(None, None, None), P(None, "dp", None)
    return jax.shard_map(
        step,
        mesh=mesh,
        in_specs=(P(("rep", "dp"), None, None, None),) * 3 + (all_of,) * 3 + (cut,) * 6,
        out_specs=(P("rep", None, None),) * 3 + (P("rep", "dp", None),) * 6,
        check_vma=False,
    )
```

time: 413 us -> 245 us (0.59)
  waiting for transfers between devices: 357 us -> 0 us
  Pallas kernels: 0 us -> 244 us
  local copies, waits for them, and re-layouts: 23.7 us -> 0 us
  other arithmetic: 17.4 us -> 0 us
  between operations: 14.1 us -> 0.66 us
    pallas_call x0 -> x3, Pallas kernels: none -> 244 us  [the longest x1 230 us: step(): pl.pallas_call(kernel, out_shape=tuple((pltpu.VMEM(one.shape, one.dtype)...]
    reduce_scatter x3 -> x0, waiting for transfers between devices: 198 us -> none  [step(): lax.psum_scatter(t[0], 'dp', scatter_dimension=1, tiled=True)]
    all_gather x3 -> x0, waiting for transfers between devices: 157 us -> none  [step(): whole = [lax.all_gather(one[0], 'dp', axis=1, tiled=True) for one in new]]
    unnamed x7 -> x0, local copies, waits for them, and re-layouts: 23.7 us -> none
    convert_element_type x3 -> x0, other arithmetic: 17.4 us -> none  [adamw(): return ((w - 0.02 * step).astype(jnp.bfloat16), m, v)]
  transfers between devices with their start and end apart: 6 -> 0, of which waited for: 6 -> 0; matrix products, arithmetic and copies ran while one was open for 4% -> 0% of each run, Pallas kernels for 0% -> 0%
where the time goes in v3:
time: 245 us
  Pallas kernels  244 us (100%)
    pallas_call x1, Pallas kernels, step(): pl.pallas_call(kernel, out_shape=tuple((pltpu.VMEM(one.shape, one.dtype)...  230 us
    pallas_call x2, Pallas kernels, to_hbm(): pl.pallas_call(functools.partial(copy_out, n), out_shape=tuple((jax.Shape...  14.1 us

profile of v3, /device:TPU:0, one launch (start us, length us, event | category | flops | bytes accessed | tf_op | source)
XLA Modules:
  0.0 245.1 jit_solution(11891014424395554415)
XLA Ops:
  0.6 230.3 %shard_map.187 = (bf16[2,896,2560]{2,1,0:T(8,128)(2,1)S(1)}, bf16[2,896,2560]{2,1,0:T(8,128)(2,1)S(1)}, bf16[2,2560,896]{2,1,0:T(8,128)(2,1)S(1)}, f32[2,112,256...) custom-call(bf16[2,896,2560]{2,1,0:T(8,128)(2,1)} %bitcast.3, ...), custom_call_target="tpu_custom_call" | custom-call | tf_op jit(solution)/shard_map/pallas_call | solution.py:253
  231.0 6.4 %shard_map.188 = (bf16[2,896,2560]{2,1,0:T(8,128)(2,1)}, bf16[2,896,2560]{2,1,0:T(8,128)(2,1)}) custom-call(bf16[2,896,2560]{2,1,0:T(8,128)(2,1)S(1)} %get-tuple-element.27.refs_0_, bf16[2,896,2560]{2,1,0:T(8,128)(2,1)S(1)} %get-tuple-element.28.refs_1_), custom_call_target="tpu_custom_call" | custom-call | tf_op jit(solution)/shard_map/pallas_call | solution.py:237
  237.4 7.7 %shard_map.189 = (bf16[2,2560,896]{2,1,0:T(8,128)(2,1)}, f32[2,112,2560]{2,1,0:T(8,128)}, f32[2,112,2560]{2,1,0:T(8,128)}, f32[2,320,896]{2,1,0:T(8,128)}, f32[2...) custom-call(bf16[2,2560,896]{2,1,0:T(8,128)(2,1)S(1)} %get-tuple-element.31.refs_0_, ...), custom_call_target="tpu_custom_call" | custom-call | tf_op jit(solution)/shard_map/pallas_call | solution.py:237
